TPU v7x, 128 devices: a whole 4x4x4 slice. The times are simulated.
128 devices in a mesh: north: 32 (over y, x, core), deep: 4 (over z).
Axes of the slice: x: 4, y: 4, z: 4, core: 2. Of those that a mesh axis runs over, the one named last changes fastest.
Arguments:
- velocity: float32 [4, 512, 256, 256], P(None, None, 'north', 'deep'), may hold values from -6 to 6
- coupling: float32 [4, 4], replicated, may hold values from -4 to 4
- symbol_x: float32 [512], replicated, may hold values from 0.3 to 3
- symbol_y: float32 [256], replicated, may hold values from 0.3 to 3
- symbol_z: float32 [256], replicated, may hold values from 0.3 to 3
Outputs:
- spectrum: float32 [4, 512, 256, 256], P(None, 'north', 'deep')
All inputs are finite; a program needn't handle non-finite values.
Results may differ from a plain program's by a relative error of at most 0.00007.
Values sent between devices are 32-bit elements; how exact they have to be, the bound alone decides.
A program may use at most 128 MiB of HBM per device.

v0:
```python
import functools

import jax
import jax.numpy as jnp
import numpy as np
from jax import lax
from jax.experimental import pallas as pl
from jax.experimental.pallas import tpu as pltpu
from jax.sharding import PartitionSpec as P

MESH = pl.DeviceIdType.MESH
F32, BF16 = jnp.float32, jnp.bfloat16
CHUNKS = 8
GROUPS = ((0, 1), (1, 3), (3, 8))


def basis_table(count):
    rank = np.arange(1, count + 1)
    turns = (rank[:, None] * rank[None, :]) % (2 * count + 2)
    return np.sin(np.pi * turns / (count + 1)) * np.sqrt(2.0 / (count + 1))


def two_parts(table):
    high = table.astype(BF16)
    low = (table - high.astype(np.float64)).astype(BF16)
    return np.stack([high, low])


def split(values):
    high = values.astype(BF16)
    return high, (values - high.astype(F32)).astype(BF16)


def dot(a, b, transposed=False):
    dims = (((1,), (1 if transposed else 0,)), ((), ()))
    return lax.dot_general(a, b, dims, preferred_element_type=F32)


def product(a_high, a_low, b_high, b_low, transposed=False):
    small = dot(a_high, b_low, transposed) + dot(a_low, b_high, transposed)
    return dot(a_high, b_high, transposed) + small


def kernel(
    nn, nd, v_hbm, hx_hbm, hy_hbm, coupling, sym_x, sym_y, sym_z, out_hbm,
    vbuf, vhi, vlo, hx, hy, sbuf, rbuf, dsend, drecv, obuf, syz,
    vsem, hsem, ssem, rsem, dssem, drsem, osem,
):
    fields, ny, nz, nx = v_hbm.shape
    chunks = sbuf.shape[0]
    share_x = nx // nn
    rows = share_x // chunks
    wide = fields * nz
    tiles = wide // 128
    full_y = nn * ny
    share_y = full_y // nd
    piece = rows * tiles * ny
    me, deep = lax.axis_index("north"), lax.axis_index("deep")

    def north_peer(i):
        my, mx, mc = me // 8, (me // 2) % 4, me % 2
        return ((my + i // 8) % 4) * 8 + ((mx + (i // 2) % 4) % 4) * 2 + (mc + i % 2) % 2

    def load_v(y):
        return pltpu.make_async_copy(v_hbm.at[:, y], vbuf.at[y], vsem.at[y])

    load_hx = pltpu.make_async_copy(hx_hbm, hx, hsem.at[0])
    load_hy = pltpu.make_async_copy(hy_hbm, hy, hsem.at[1])
    load_hx.start()
    for y in range(ny):
        load_v(y).start()
    load_hy.start()

    barrier = pltpu.get_barrier_semaphore()

    @pl.loop(1, nn)
    def _(i):
        pl.semaphore_signal(
            barrier, inc=1, device_id={"north": north_peer(i), "deep": deep}, device_id_type=MESH
        )

    for i in range(1, nd):
        pl.semaphore_signal(
            barrier, inc=1, device_id={"north": me, "deep": (deep + i) % nd}, device_id_type=MESH
        )

    lane = lax.broadcasted_iota(jnp.int32, (share_y, full_y), 1)
    row = lax.broadcasted_iota(jnp.int32, (share_y, full_y), 0)
    mine = jnp.where(lane == row + deep * share_y, sym_y[...], 0.0)
    syz[...] = jnp.sum(mine, axis=1, keepdims=True) + sym_z[...]

    def transform_x(y, first, last):
        span = nn * rows
        pick = pl.ds(first * span, (last - first) * span)
        result = product(
            hx[0, pick, :], hx[1, pick, :], vhi[y], vlo[y], transposed=True
        )
        for c in range(first, last):
            part = result[(c - first) * span : (c - first + 1) * span]
            for t in range(tiles):
                sbuf[c, pl.ds(t * ny + y, span, stride=tiles * ny), :] = part[:, t * 128 : (t + 1) * 128]

    def send_north(c):
        @pl.loop(1, nn)
        def _(i):
            peer = north_peer(i)
            pltpu.make_async_remote_copy(
                src_ref=sbuf.at[c, pl.ds(pl.multiple_of(peer * piece, piece), piece)],
                dst_ref=rbuf.at[c, me],
                send_sem=ssem.at[c],
                recv_sem=rsem.at[c],
                device_id={"north": peer, "deep": deep},
                device_id_type=MESH,
            ).start()

        rbuf[c, me] = sbuf[c, pl.ds(pl.multiple_of(me * piece, piece), piece), :]

    def all_north(c):
        return pltpu.make_async_remote_copy(
            src_ref=rbuf.at[c, pl.ds(0, nn - 1)],
            dst_ref=rbuf.at[c, pl.ds(0, nn - 1)],
            send_sem=ssem.at[c],
            recv_sem=rsem.at[c],
            device_id={"north": me, "deep": deep},
            device_id_type=MESH,
        )

    def all_deep(c):
        return pltpu.make_async_remote_copy(
            src_ref=drecv.at[c, pl.ds(0, nd - 1)],
            dst_ref=drecv.at[c, pl.ds(0, nd - 1)],
            send_sem=dssem.at[c],
            recv_sem=drsem.at[c],
            device_id={"north": me, "deep": deep},
            device_id_type=MESH,
        )

    load_hx.wait()
    for y in range(ny):
        load_v(y).wait()
        high, low = split(vbuf[y].reshape(wide, nx))
        vhi[y] = high
        vlo[y] = low
        transform_x(y, *GROUPS[0])
    pl.semaphore_wait(barrier, nn - 1 + nd - 1)
    for first, last in GROUPS:
        if first > 0:
            @pl.loop(0, ny)
            def _(y):
                transform_x(y, first, last)

        for c in range(first, last):
            send_north(c)
    load_hy.wait()

    def stage_y(c):
        all_north(c).wait_recv()
        for j in range(rows):
            columns = [
                rbuf[c, :, pl.ds((j * tiles + t) * ny, ny), :].reshape(full_y, 128) for t in range(tiles)
            ]
            high, low = split(jnp.concatenate(columns, axis=1))
            result = product(hy[0], hy[1], high, low)
            for d in range(nd):
                dsend[c, d, j] = result[d * share_y : (d + 1) * share_y]
        for i in range(1, nd):
            peer = (deep + i) % nd
            pltpu.make_async_remote_copy(
                src_ref=dsend.at[c, peer],
                dst_ref=drecv.at[c, deep],
                send_sem=dssem.at[c],
                recv_sem=drsem.at[c],
                device_id={"north": me, "deep": peer},
                device_id_type=MESH,
            ).start()
        drecv[c, deep] = dsend[c, deep]

    lower = lax.broadcasted_iota(jnp.int32, (share_y, 128), 1) < nz

    def copy_out(c):
        return pltpu.make_async_copy(
            obuf.at[:, pl.ds(c * rows, rows)], out_hbm.at[:, pl.ds(c * rows, rows)], osem.at[c]
        )

    def stage_z(c):
        all_deep(c).wait_recv()
        for j in range(rows):
            lines = []
            for t in range(tiles):
                parts = [drecv[c, d, j, :, t * 128 : (t + 1) * 128] for d in range(nd)]
                turned = [pltpu.roll(p, nz, 1) for p in parts]
                even = [jnp.where(lower, parts[d], turned[d + 1]) for d in range(0, nd, 2)]
                odd = [jnp.where(lower, turned[d], parts[d + 1]) for d in range(0, nd, 2)]
                lines.append(jnp.concatenate(even, axis=1))
                lines.append(jnp.concatenate(odd, axis=1))
            high, low = split(jnp.concatenate(lines, axis=0))
            result = product(high, low, hy[0], hy[1])
            old = [result[f * share_y : (f + 1) * share_y] for f in range(fields)]
            x = c * rows + j
            weight = 1.0 / (1.0 + (sym_x[me * share_x + x] + syz[...]))
            rest = 1.0 - weight
            for a in range(fields):
                mixed = coupling[a, 0] * old[0]
                for b in range(1, fields):
                    mixed = mixed + coupling[a, b] * old[b]
                obuf[a, x] = weight * old[a] + rest * mixed
        copy_out(c).start()

    stage_y(0)

    @pl.loop(1, chunks)
    def _(c):
        stage_y(c)
        stage_z(c - 1)

    stage_z(chunks - 1)

    @pl.loop(0, chunks)
    def _(c):
        all_north(c).wait_send()
        all_deep(c).wait_send()
        copy_out(c).wait()


def on_device(nn, nd, velocity, coupling, symbol_x, symbol_y, symbol_z):
    fields, nx, ny, nz = velocity.shape
    share_x = nx // nn
    rows = share_x // CHUNKS
    full_y, full_z = ny * nn, nz * nd
    share_y = full_y // nd
    wide = fields * nz
    tiles = wide // 128
    order = np.arange(nx).reshape(nn, CHUNKS, rows).transpose(1, 0, 2).reshape(-1)
    table_x = jnp.asarray(two_parts(basis_table(nx)[order]))
    table_y = jnp.asarray(two_parts(basis_table(full_y)))
    anywhere = pl.BlockSpec(memory_space=pl.ANY)
    scalars = pl.BlockSpec(memory_space=pltpu.SMEM)
    vector = pl.BlockSpec(memory_space=pltpu.VMEM)
    dma = pltpu.SemaphoreType.DMA
    return pl.pallas_call(
        functools.partial(kernel, nn, nd),
        out_shape=jax.ShapeDtypeStruct((fields, share_x, share_y, full_z), F32),
        in_specs=[anywhere, anywhere, anywhere, scalars, scalars, vector, vector],
        out_specs=anywhere,
        scratch_shapes=[
            pltpu.VMEM((ny, fields, nz, nx), F32),
            pltpu.VMEM((ny, wide, nx), BF16),
            pltpu.VMEM((ny, wide, nx), BF16),
            pltpu.VMEM((2, nx, nx), BF16),
            pltpu.VMEM((2, full_y, full_y), BF16),
            pltpu.VMEM((CHUNKS, nn * rows * tiles * ny, 128), F32),
            pltpu.VMEM((CHUNKS, nn, rows * tiles * ny, 128), F32),
            pltpu.VMEM((CHUNKS, nd, rows, share_y, wide), F32),
            pltpu.VMEM((CHUNKS, nd, rows, share_y, wide), F32),
            pltpu.VMEM((fields, share_x, share_y, full_z), F32),
            pltpu.VMEM((share_y, full_z), F32),
            dma((ny,)), dma((2,)),
            dma((CHUNKS,)), dma((CHUNKS,)), dma((CHUNKS,)), dma((CHUNKS,)), dma((CHUNKS,)),
        ],
        compiler_params=pltpu.CompilerParams(
            collective_id=0, has_side_effects=True, vmem_limit_bytes=56 << 20
        ),
    )(
        jnp.transpose(velocity, (0, 2, 3, 1)), table_x, table_y, coupling, symbol_x,
        symbol_y.reshape(1, full_y), symbol_z.reshape(1, full_z),
    )


def solution(mesh):
    placed = (P(None, None, "north", "deep"), P(), P(), P(), P())
    return jax.shard_map(
        functools.partial(on_device, mesh.shape["north"], mesh.shape["deep"]),
        mesh=mesh,
        in_specs=placed,
        out_specs=P(None, "north", "deep", None),
        check_vma=False,
    )
```

profile of v0, /device:TPU:0, one launch (start us, length us, event | category | flops | bytes accessed | tf_op | source)
XLA Modules:
  0.0 79.2 jit_solution(6763081263410161375)
XLA Ops:
  0.0 74.5 %shard_map.73 = f32[4,16,64,256]{3,2,1,0:T(8,128)} custom-call(f32[4,8,64,512]{3,2,1,0:T(8,128)} %bitcast.3, bf16[2,512,512]{2,1,0:T(8,128)(2,1)} %constant.4.clone.hx_hbm, bf16[2,256,256]{2,1,0:T(8,128)(2,1)} %constant.5.clone.hy_hbm, f32[4,4]{1,0:T(4,128)} %coupling.1, f32[512]{0:T(512)} %sym_x.1, f32[1,256]{1,0:T(1,128)} %bitcast.4, f32[1,256]{1,0:T(1,128)} %bitcast.5), custom_call_target="tpu_custom_call" | custom-call | tf_op jit(solution)/shard_map/pallas_call | solution.py:240
  74.5 4.7 %copy.9 = f32[4,16,64,256]{3,2,1,0:T(8,128)} copy(f32[4,16,64,256]{3,2,1,0:T(8,128)} %shard_map.73) | data formatting | bytes 8388608
where the time goes:
time: 79.5 us; the launch traced here: 79.2 us
  Pallas kernels  74.5 us (94%)
  local copies, waits for them, and re-layouts  4.7 us (6%)
    pallas_call x1, Pallas kernels, on_device(): pl.pallas_call(functools.partial(kernel, nn, nd), out_shape=jax.ShapeDtyp...  74.5 us
    unnamed x1, local copies, waits for them, and re-layouts  4.7 us

commit v1 on v0

--- a/solution.py
+++ b/solution.py
@@ -10,8 +10,8 @@
 
 MESH = pl.DeviceIdType.MESH
 F32, BF16 = jnp.float32, jnp.bfloat16
-CHUNKS = 8
-GROUPS = ((0, 1), (1, 3), (3, 8))
+CHUNKS = 16
+GROUPS = ((0, 2), (2, 8), (8, 16))
 
 
 def basis_table(count):
@@ -37,14 +37,15 @@
 
 
 def product(a_high, a_low, b_high, b_low, transposed=False):
-    small = dot(a_high, b_low, transposed) + dot(a_low, b_high, transposed)
-    return dot(a_high, b_high, transposed) + small
+    count = a_high.shape[0]
+    both = dot(jnp.concatenate([a_high, a_low], axis=0), b_high, transposed)
+    return both[:count] + (both[count:] + dot(a_high, b_low, transposed))
 
 
 def kernel(
-    nn, nd, v_hbm, hx_hbm, hy_hbm, coupling, sym_x, sym_y, sym_z, out_hbm,
-    vbuf, vhi, vlo, hx, hy, sbuf, rbuf, dsend, drecv, obuf, syz,
-    vsem, hsem, ssem, rsem, dssem, drsem, osem,
+    nn, nd, v_hbm, hx_hbm, hy_hbm, coupling_hbm, sym_x_hbm, sym_y_hbm, sym_z_hbm, out,
+    vbuf, vhi, vlo, hx, hy, sbuf, rbuf, dsend, drecv, syz, coupling, sym_x, sym_y, sym_z,
+    vsem, hsem, ssem, rsem, dssem, drsem,
 ):
     fields, ny, nz, nx = v_hbm.shape
     chunks = sbuf.shape[0]
@@ -57,53 +58,48 @@
     piece = rows * tiles * ny
     me, deep = lax.axis_index("north"), lax.axis_index("deep")
 
-    def north_peer(i):
-        my, mx, mc = me // 8, (me // 2) % 4, me % 2
-        return ((my + i // 8) % 4) * 8 + ((mx + (i // 2) % 4) % 4) * 2 + (mc + i % 2) % 2
-
-    def load_v(y):
-        return pltpu.make_async_copy(v_hbm.at[:, y], vbuf.at[y], vsem.at[y])
-
-    load_hx = pltpu.make_async_copy(hx_hbm, hx, hsem.at[0])
-    load_hy = pltpu.make_async_copy(hy_hbm, hy, hsem.at[1])
-    load_hx.start()
-    for y in range(ny):
-        load_v(y).start()
-    load_hy.start()
+    loads = [
+        pltpu.make_async_copy(a, b, hsem.at[k])
+        for k, (a, b) in enumerate((
+            (hx_hbm, hx), (hy_hbm, hy), (coupling_hbm, coupling), (sym_x_hbm, sym_x),
+            (sym_y_hbm, sym_y), (sym_z_hbm, sym_z),
+        ))
+    ]
+    load_v = [pltpu.make_async_copy(v_hbm.at[:, y], vbuf.at[y], vsem.at[y]) for y in range(ny)]
+    loads[0].start()
+    for copy in load_v:
+        copy.start()
+    for copy in loads[1:]:
+        copy.start()
+
+    along_y = [lax.rem(me // 8 + i, 4) * 8 for i in range(4)]
+    along_x = [lax.rem(me // 2 + i, 4) * 2 for i in range(4)]
+    cores = [lax.rem(me + i, 2) for i in range(2)]
+    steps = [(a, b, c) for a in range(4) for b in range(4) for c in range(2)][1:]
+    others = [along_y[a] + along_x[b] + cores[c] for a, b, c in steps]
+    above = [lax.rem(deep + i, nd) for i in range(1, nd)]
 
     barrier = pltpu.get_barrier_semaphore()
-
-    @pl.loop(1, nn)
-    def _(i):
+    for peer in others:
         pl.semaphore_signal(
-            barrier, inc=1, device_id={"north": north_peer(i), "deep": deep}, device_id_type=MESH
-        )
-
-    for i in range(1, nd):
+            barrier, inc=1, device_id={"north": peer, "deep": deep}, device_id_type=MESH
+        )
+    for peer in above:
         pl.semaphore_signal(
-            barrier, inc=1, device_id={"north": me, "deep": (deep + i) % nd}, device_id_type=MESH
-        )
-
-    lane = lax.broadcasted_iota(jnp.int32, (share_y, full_y), 1)
-    row = lax.broadcasted_iota(jnp.int32, (share_y, full_y), 0)
-    mine = jnp.where(lane == row + deep * share_y, sym_y[...], 0.0)
-    syz[...] = jnp.sum(mine, axis=1, keepdims=True) + sym_z[...]
-
-    def transform_x(y, first, last):
+            barrier, inc=1, device_id={"north": me, "deep": peer}, device_id_type=MESH
+        )
+
+    def transform_x(y, first, last, high, low):
         span = nn * rows
         pick = pl.ds(first * span, (last - first) * span)
-        result = product(
-            hx[0, pick, :], hx[1, pick, :], vhi[y], vlo[y], transposed=True
-        )
+        result = product(hx[0, pick, :], hx[1, pick, :], high, low, transposed=True)
         for c in range(first, last):
             part = result[(c - first) * span : (c - first + 1) * span]
             for t in range(tiles):
                 sbuf[c, pl.ds(t * ny + y, span, stride=tiles * ny), :] = part[:, t * 128 : (t + 1) * 128]
 
     def send_north(c):
-        @pl.loop(1, nn)
-        def _(i):
-            peer = north_peer(i)
+        for peer in others:
             pltpu.make_async_remote_copy(
                 src_ref=sbuf.at[c, pl.ds(pl.multiple_of(peer * piece, piece), piece)],
                 dst_ref=rbuf.at[c, me],
@@ -112,7 +108,6 @@
                 device_id={"north": peer, "deep": deep},
                 device_id_type=MESH,
             ).start()
-
         rbuf[c, me] = sbuf[c, pl.ds(pl.multiple_of(me * piece, piece), piece), :]
 
     def all_north(c):
@@ -135,23 +130,14 @@
             device_id_type=MESH,
         )
 
-    load_hx.wait()
-    for y in range(ny):
-        load_v(y).wait()
-        high, low = split(vbuf[y].reshape(wide, nx))
-        vhi[y] = high
-        vlo[y] = low
-        transform_x(y, *GROUPS[0])
-    pl.semaphore_wait(barrier, nn - 1 + nd - 1)
-    for first, last in GROUPS:
-        if first > 0:
-            @pl.loop(0, ny)
-            def _(y):
-                transform_x(y, first, last)
-
-        for c in range(first, last):
+    def group_x(first, last):
+        @pl.loop(0, ny)
+        def _(y):
+            transform_x(y, first, last, vhi[y], vlo[y])
+
+        @pl.loop(first, last)
+        def _(c):
             send_north(c)
-    load_hy.wait()
 
     def stage_y(c):
         all_north(c).wait_recv()
@@ -163,8 +149,7 @@
             result = product(hy[0], hy[1], high, low)
             for d in range(nd):
                 dsend[c, d, j] = result[d * share_y : (d + 1) * share_y]
-        for i in range(1, nd):
-            peer = (deep + i) % nd
+        for peer in above:
             pltpu.make_async_remote_copy(
                 src_ref=dsend.at[c, peer],
                 dst_ref=drecv.at[c, deep],
@@ -176,11 +161,6 @@
         drecv[c, deep] = dsend[c, deep]
 
     lower = lax.broadcasted_iota(jnp.int32, (share_y, 128), 1) < nz
-
-    def copy_out(c):
-        return pltpu.make_async_copy(
-            obuf.at[:, pl.ds(c * rows, rows)], out_hbm.at[:, pl.ds(c * rows, rows)], osem.at[c]
-        )
 
     def stage_z(c):
         all_deep(c).wait_recv()
@@ -203,10 +183,32 @@
                 mixed = coupling[a, 0] * old[0]
                 for b in range(1, fields):
                     mixed = mixed + coupling[a, b] * old[b]
-                obuf[a, x] = weight * old[a] + rest * mixed
-        copy_out(c).start()
-
+                out[a, x] = weight * old[a] + rest * mixed
+
+    loads[0].wait()
+    for copy in load_v:
+        copy.wait()
+    for y in range(ny):
+        high, low = split(vbuf[y].reshape(wide, nx))
+        vhi[y] = high
+        vlo[y] = low
+        transform_x(y, *GROUPS[0], high, low)
+    pl.semaphore_wait(barrier, nn - 1 + nd - 1)
+
+    @pl.loop(*GROUPS[0])
+    def _(c):
+        send_north(c)
+
+    group_x(*GROUPS[1])
+    for copy in loads[1:]:
+        copy.wait()
     stage_y(0)
+    group_x(*GROUPS[2])
+
+    lane = lax.broadcasted_iota(jnp.int32, (share_y, full_y), 1)
+    row = lax.broadcasted_iota(jnp.int32, (share_y, full_y), 0)
+    mine = jnp.where(lane == row + deep * share_y, sym_y[...], 0.0)
+    syz[...] = jnp.sum(mine, axis=1, keepdims=True) + sym_z[...]
 
     @pl.loop(1, chunks)
     def _(c):
@@ -219,7 +221,6 @@
     def _(c):
         all_north(c).wait_send()
         all_deep(c).wait_send()
-        copy_out(c).wait()
 
 
 def on_device(nn, nd, velocity, coupling, symbol_x, symbol_y, symbol_z):
@@ -233,15 +234,12 @@
     order = np.arange(nx).reshape(nn, CHUNKS, rows).transpose(1, 0, 2).reshape(-1)
     table_x = jnp.asarray(two_parts(basis_table(nx)[order]))
     table_y = jnp.asarray(two_parts(basis_table(full_y)))
-    anywhere = pl.BlockSpec(memory_space=pl.ANY)
-    scalars = pl.BlockSpec(memory_space=pltpu.SMEM)
-    vector = pl.BlockSpec(memory_space=pltpu.VMEM)
     dma = pltpu.SemaphoreType.DMA
     return pl.pallas_call(
         functools.partial(kernel, nn, nd),
         out_shape=jax.ShapeDtypeStruct((fields, share_x, share_y, full_z), F32),
-        in_specs=[anywhere, anywhere, anywhere, scalars, scalars, vector, vector],
-        out_specs=anywhere,
+        in_specs=[pl.BlockSpec(memory_space=pltpu.MemorySpace.HBM)] * 7,
+        out_specs=pl.BlockSpec(memory_space=pltpu.VMEM),
         scratch_shapes=[
             pltpu.VMEM((ny, fields, nz, nx), F32),
             pltpu.VMEM((ny, wide, nx), BF16),
@@ -252,18 +250,24 @@
             pltpu.VMEM((CHUNKS, nn, rows * tiles * ny, 128), F32),
             pltpu.VMEM((CHUNKS, nd, rows, share_y, wide), F32),
             pltpu.VMEM((CHUNKS, nd, rows, share_y, wide), F32),
-            pltpu.VMEM((fields, share_x, share_y, full_z), F32),
             pltpu.VMEM((share_y, full_z), F32),
-            dma((ny,)), dma((2,)),
-            dma((CHUNKS,)), dma((CHUNKS,)), dma((CHUNKS,)), dma((CHUNKS,)), dma((CHUNKS,)),
+            pltpu.SMEM((fields, fields), F32),
+            pltpu.SMEM((nx,), F32),
+            pltpu.VMEM((1, full_y), F32),
+            pltpu.VMEM((1, full_z), F32),
+            dma((ny,)), dma((6,)),
+            dma((CHUNKS,)), dma((CHUNKS,)), dma((CHUNKS,)), dma((CHUNKS,)),
         ],
         compiler_params=pltpu.CompilerParams(
-            collective_id=0, has_side_effects=True, vmem_limit_bytes=56 << 20
+            collective_id=0, has_side_effects=True, vmem_limit_bytes=32 << 20
         ),
-    )(
-        jnp.transpose(velocity, (0, 2, 3, 1)), table_x, table_y, coupling, symbol_x,
-        symbol_y.reshape(1, full_y), symbol_z.reshape(1, full_z),
-    )
+    )(*(
+        pltpu.with_memory_space_constraint(array, pltpu.MemorySpace.HBM)
+        for array in (
+            jnp.transpose(velocity, (0, 2, 3, 1)), table_x, table_y, coupling, symbol_x,
+            symbol_y.reshape(1, full_y), symbol_z.reshape(1, full_z),
+        )
+    ))
 
 
 def solution(mesh):

time: 79.5 us -> 74.7 us (0.940)
  local copies, waits for them, and re-layouts: 4.7 us -> 2.02 us
  Pallas kernels: 74.5 us -> 72.6 us
    unnamed x1, local copies, waits for them, and re-layouts: 4.7 us -> 2.02 us
    pallas_call x1, Pallas kernels: 74.5 us -> 72.6 us  [on_device(): pl.pallas_call(functools.partial(kernel, nn, nd), out_shape=jax.ShapeDtyp...]
where the time goes in v1:
time: 74.7 us; the launch traced here: 74.6 us
  Pallas kernels  72.6 us (97%)
  local copies, waits for them, and re-layouts  2.02 us (3%)
    pallas_call x1, Pallas kernels, on_device(): pl.pallas_call(functools.partial(kernel, nn, nd), out_shape=jax.ShapeDtyp...  72.6 us
    unnamed x1, local copies, waits for them, and re-layouts  2.02 us

profile of v1, /device:TPU:0, one launch (start us, length us, event | category | flops | bytes accessed | tf_op | source)
XLA Modules:
  0.0 74.6 jit_solution(4605127653385854523)
XLA Ops:
  0.0 72.6 %shard_map.73 = f32[4,16,64,256]{3,2,1,0:T(8,128)S(1)} custom-call(f32[4,8,64,512]{3,2,1,0:T(8,128)} %bitcast.3, bf16[2,512,512]{2,1,0:T(8,128)(2,1)} %constant.4.clone.hx_hbm, bf16[2,256,256]{2,1,0:T(8,128)(2,1)} %constant.5.clone.hy_hbm, f32[4,4]{1,0:T(4,128)} %coupling_hbm.1, f32[512]{0:T(512)} %sym_x_hbm.1, f32[1,256]{1,0:T(1,128)} %bitcast.4, ...), custom_call_target="tpu_custom_call" | custom-call | tf_op jit(solution)/shard_map/pallas_call | solution.py:238
  72.6 2.0 %copy.9 = f32[4,16,64,256]{3,2,1,0:T(8,128)} copy(f32[4,16,64,256]{3,2,1,0:T(8,128)S(1)} %shard_map.73) | data formatting | bytes 8388608

commit v2 on v1

--- a/solution.py
+++ b/solution.py
@@ -11,7 +11,9 @@
 MESH = pl.DeviceIdType.MESH
 F32, BF16 = jnp.float32, jnp.bfloat16
 CHUNKS = 16
-GROUPS = ((0, 2), (2, 8), (8, 16))
+FIRST = 2
+PLAN = ((2, 8), "start", (8, 11), 1, (11, 14), 2, (14, 16))
+LAG = 4
 
 
 def basis_table(count):
@@ -55,7 +57,7 @@
     tiles = wide // 128
     full_y = nn * ny
     share_y = full_y // nd
-    piece = rows * tiles * ny
+    piece = rows * ny
     me, deep = lax.axis_index("north"), lax.axis_index("deep")
 
     loads = [
@@ -69,8 +71,6 @@
     loads[0].start()
     for copy in load_v:
         copy.start()
-    for copy in loads[1:]:
-        copy.start()
 
     along_y = [lax.rem(me // 8 + i, 4) * 8 for i in range(4)]
     along_x = [lax.rem(me // 2 + i, 4) * 2 for i in range(4)]
@@ -96,39 +96,47 @@
         for c in range(first, last):
             part = result[(c - first) * span : (c - first + 1) * span]
             for t in range(tiles):
-                sbuf[c, pl.ds(t * ny + y, span, stride=tiles * ny), :] = part[:, t * 128 : (t + 1) * 128]
-
-    def send_north(c):
-        for peer in others:
-            pltpu.make_async_remote_copy(
-                src_ref=sbuf.at[c, pl.ds(pl.multiple_of(peer * piece, piece), piece)],
-                dst_ref=rbuf.at[c, me],
-                send_sem=ssem.at[c],
-                recv_sem=rsem.at[c],
+                sbuf[c, t, pl.ds(y, span, stride=ny), :] = part[:, t * 128 : (t + 1) * 128]
+
+    def north(c, slot, tile, start):
+        pick = pl.ds(0, tiles) if tile is None else pl.ds(tile, 1)
+
+        def copy(source, target, peer):
+            return pltpu.make_async_remote_copy(
+                src_ref=source,
+                dst_ref=target,
+                send_sem=ssem.at[slot],
+                recv_sem=rsem.at[slot],
                 device_id={"north": peer, "deep": deep},
                 device_id_type=MESH,
-            ).start()
-        rbuf[c, me] = sbuf[c, pl.ds(pl.multiple_of(me * piece, piece), piece), :]
-
-    def all_north(c):
-        return pltpu.make_async_remote_copy(
-            src_ref=rbuf.at[c, pl.ds(0, nn - 1)],
-            dst_ref=rbuf.at[c, pl.ds(0, nn - 1)],
-            send_sem=ssem.at[c],
-            recv_sem=rsem.at[c],
-            device_id={"north": me, "deep": deep},
-            device_id_type=MESH,
-        )
-
-    def all_deep(c):
-        return pltpu.make_async_remote_copy(
-            src_ref=drecv.at[c, pl.ds(0, nd - 1)],
-            dst_ref=drecv.at[c, pl.ds(0, nd - 1)],
-            send_sem=dssem.at[c],
-            recv_sem=drsem.at[c],
-            device_id={"north": me, "deep": deep},
-            device_id_type=MESH,
-        )
+            )
+
+        if not start:
+            everything = rbuf.at[c, pick, pl.ds(0, nn - 1)]
+            return copy(everything, everything, me)
+        for peer in others:
+            copy(sbuf.at[c, pick, pl.ds(pl.multiple_of(peer * piece, piece), piece)], rbuf.at[c, pick, me], peer).start()
+        rbuf[c, pick, me] = sbuf[c, pick, pl.ds(pl.multiple_of(me * piece, piece), piece), :]
+
+    def vertical(c, slot, tile, start):
+        pick = pl.ds(0, tiles) if tile is None else pl.ds(tile, 1)
+
+        def copy(source, target, peer):
+            return pltpu.make_async_remote_copy(
+                src_ref=source,
+                dst_ref=target,
+                send_sem=dssem.at[slot],
+                recv_sem=drsem.at[slot],
+                device_id={"north": me, "deep": peer},
+                device_id_type=MESH,
+            )
+
+        if not start:
+            everything = drecv.at[c, pl.ds(0, nd - 1), pick]
+            return copy(everything, everything, deep)
+        for peer in above:
+            copy(dsend.at[c, peer, pick], drecv.at[c, deep, pick], peer).start()
+        drecv[c, deep, pick] = dsend[c, deep, pick]
 
     def group_x(first, last):
         @pl.loop(0, ny)
@@ -137,37 +145,27 @@
 
         @pl.loop(first, last)
         def _(c):
-            send_north(c)
-
-    def stage_y(c):
-        all_north(c).wait_recv()
+            north(c, c, None, True)
+
+    def stage_y(c, slot, tile=None):
+        north(c, slot, tile, False).wait_recv()
+        span = range(tiles) if tile is None else (tile,)
         for j in range(rows):
-            columns = [
-                rbuf[c, :, pl.ds((j * tiles + t) * ny, ny), :].reshape(full_y, 128) for t in range(tiles)
-            ]
+            columns = [rbuf[c, t, :, pl.ds(j * ny, ny), :].reshape(full_y, 128) for t in span]
             high, low = split(jnp.concatenate(columns, axis=1))
             result = product(hy[0], hy[1], high, low)
             for d in range(nd):
-                dsend[c, d, j] = result[d * share_y : (d + 1) * share_y]
-        for peer in above:
-            pltpu.make_async_remote_copy(
-                src_ref=dsend.at[c, peer],
-                dst_ref=drecv.at[c, deep],
-                send_sem=dssem.at[c],
-                recv_sem=drsem.at[c],
-                device_id={"north": me, "deep": peer},
-                device_id_type=MESH,
-            ).start()
-        drecv[c, deep] = dsend[c, deep]
+                for k, t in enumerate(span):
+                    dsend[c, d, t, j] = result[d * share_y : (d + 1) * share_y, k * 128 : (k + 1) * 128]
+        vertical(c, slot, tile, True)
 
     lower = lax.broadcasted_iota(jnp.int32, (share_y, 128), 1) < nz
 
     def stage_z(c):
-        all_deep(c).wait_recv()
         for j in range(rows):
             lines = []
             for t in range(tiles):
-                parts = [drecv[c, d, j, :, t * 128 : (t + 1) * 128] for d in range(nd)]
+                parts = [drecv[c, d, t, j] for d in range(nd)]
                 turned = [pltpu.roll(p, nz, 1) for p in parts]
                 even = [jnp.where(lower, parts[d], turned[d + 1]) for d in range(0, nd, 2)]
                 odd = [jnp.where(lower, turned[d], parts[d + 1]) for d in range(0, nd, 2)]
@@ -186,41 +184,69 @@
                 out[a, x] = weight * old[a] + rest * mixed
 
     loads[0].wait()
-    for copy in load_v:
-        copy.wait()
-    for y in range(ny):
-        high, low = split(vbuf[y].reshape(wide, nx))
-        vhi[y] = high
-        vlo[y] = low
-        transform_x(y, *GROUPS[0], high, low)
+    for y in range(0, ny, 2):
+        load_v[y].wait()
+        load_v[y + 1].wait()
+        for k in (y, y + 1):
+            high, low = split(vbuf[k].reshape(wide, nx))
+            vhi[k] = high
+            vlo[k] = low
+            transform_x(k, 0, FIRST, high, low)
+    for copy in loads[1:]:
+        copy.start()
     pl.semaphore_wait(barrier, nn - 1 + nd - 1)
-
-    @pl.loop(*GROUPS[0])
-    def _(c):
-        send_north(c)
-
-    group_x(*GROUPS[1])
-    for copy in loads[1:]:
-        copy.wait()
-    stage_y(0)
-    group_x(*GROUPS[2])
+    north(0, 0, 0, True)
+    north(0, chunks, 1, True)
+    for c in range(1, FIRST):
+        north(c, c, None, True)
+
+    done = 1
+    for item in PLAN:
+        if item == "start":
+            for copy in loads[1:]:
+                copy.wait()
+            stage_y(0, 0, 0)
+            stage_y(0, chunks, 1)
+        elif isinstance(item, tuple):
+            group_x(*item)
+        else:
+            stage_y(item, item)
+            done = item + 1
 
     lane = lax.broadcasted_iota(jnp.int32, (share_y, full_y), 1)
     row = lax.broadcasted_iota(jnp.int32, (share_y, full_y), 0)
     mine = jnp.where(lane == row + deep * share_y, sym_y[...], 0.0)
     syz[...] = jnp.sum(mine, axis=1, keepdims=True) + sym_z[...]
 
+    @pl.loop(done, LAG)
+    def _(c):
+        stage_y(c, c)
+
+    vertical(0, 0, 0, False).wait_recv()
+    vertical(0, chunks, 1, False).wait_recv()
+    stage_y(LAG, LAG)
+    stage_z(0)
+
+    @pl.loop(LAG + 1, chunks)
+    def _(c):
+        stage_y(c, c)
+        vertical(c - LAG, c - LAG, None, False).wait_recv()
+        stage_z(c - LAG)
+
+    @pl.loop(chunks - LAG, chunks)
+    def _(c):
+        vertical(c, c, None, False).wait_recv()
+        stage_z(c)
+
+    north(0, 0, 0, False).wait_send()
+    north(0, chunks, 1, False).wait_send()
+    vertical(0, 0, 0, False).wait_send()
+    vertical(0, chunks, 1, False).wait_send()
+
     @pl.loop(1, chunks)
     def _(c):
-        stage_y(c)
-        stage_z(c - 1)
-
-    stage_z(chunks - 1)
-
-    @pl.loop(0, chunks)
-    def _(c):
-        all_north(c).wait_send()
-        all_deep(c).wait_send()
+        north(c, c, None, False).wait_send()
+        vertical(c, c, None, False).wait_send()
 
 
 def on_device(nn, nd, velocity, coupling, symbol_x, symbol_y, symbol_z):
@@ -246,17 +272,17 @@
             pltpu.VMEM((ny, wide, nx), BF16),
             pltpu.VMEM((2, nx, nx), BF16),
             pltpu.VMEM((2, full_y, full_y), BF16),
-            pltpu.VMEM((CHUNKS, nn * rows * tiles * ny, 128), F32),
-            pltpu.VMEM((CHUNKS, nn, rows * tiles * ny, 128), F32),
-            pltpu.VMEM((CHUNKS, nd, rows, share_y, wide), F32),
-            pltpu.VMEM((CHUNKS, nd, rows, share_y, wide), F32),
+            pltpu.VMEM((CHUNKS, tiles, nn * rows * ny, 128), F32),
+            pltpu.VMEM((CHUNKS, tiles, nn, rows * ny, 128), F32),
+            pltpu.VMEM((CHUNKS, nd, tiles, rows, share_y, 128), F32),
+            pltpu.VMEM((CHUNKS, nd, tiles, rows, share_y, 128), F32),
             pltpu.VMEM((share_y, full_z), F32),
             pltpu.SMEM((fields, fields), F32),
             pltpu.SMEM((nx,), F32),
             pltpu.VMEM((1, full_y), F32),
             pltpu.VMEM((1, full_z), F32),
             dma((ny,)), dma((6,)),
-            dma((CHUNKS,)), dma((CHUNKS,)), dma((CHUNKS,)), dma((CHUNKS,)),
+            dma((CHUNKS + 1,)), dma((CHUNKS + 1,)), dma((CHUNKS + 1,)), dma((CHUNKS + 1,)),
         ],
         compiler_params=pltpu.CompilerParams(
             collective_id=0, has_side_effects=True, vmem_limit_bytes=32 << 20

time: 74.7 us -> 69.2 us (0.926)
  Pallas kernels: 72.6 us -> 66.9 us
    pallas_call x1, Pallas kernels: 72.6 us -> 66.9 us  [on_device(): pl.pallas_call(functools.partial(kernel, nn, nd), out_shape=jax.ShapeDtyp...]
where the time goes in v2:
time: 69.2 us; the launch traced here: 68.9 us
  Pallas kernels  66.9 us (97%)
  local copies, waits for them, and re-layouts  2.02 us (3%)
    pallas_call x1, Pallas kernels, on_device(): pl.pallas_call(functools.partial(kernel, nn, nd), out_shape=jax.ShapeDtyp...  66.9 us
    unnamed x1, local copies, waits for them, and re-layouts  2.02 us

profile of v2, /device:TPU:0, one launch (start us, length us, event | category | flops | bytes accessed | tf_op | source)
XLA Modules:
  0.0 68.9 jit_solution(7982941830332704471)
XLA Ops:
  0.0 66.9 %shard_map.73 = f32[4,16,64,256]{3,2,1,0:T(8,128)S(1)} custom-call(f32[4,8,64,512]{3,2,1,0:T(8,128)} %bitcast.3, bf16[2,512,512]{2,1,0:T(8,128)(2,1)} %constant.4.clone.hx_hbm, bf16[2,256,256]{2,1,0:T(8,128)(2,1)} %constant.5.clone.hy_hbm, f32[4,4]{1,0:T(4,128)} %coupling_hbm.1, f32[512]{0:T(512)} %sym_x_hbm.1, f32[1,256]{1,0:T(1,128)} %bitcast.4, ...), custom_call_target="tpu_custom_call" | custom-call | tf_op jit(solution)/shard_map/pallas_call | solution.py:264
  66.9 2.0 %copy.9 = f32[4,16,64,256]{3,2,1,0:T(8,128)} copy(f32[4,16,64,256]{3,2,1,0:T(8,128)S(1)} %shard_map.73) | data formatting | bytes 8388608

commit v3 on v2

--- a/solution.py
+++ b/solution.py
@@ -11,9 +11,10 @@
 MESH = pl.DeviceIdType.MESH
 F32, BF16 = jnp.float32, jnp.bfloat16
 CHUNKS = 16
-FIRST = 2
-PLAN = ((2, 8), "start", (8, 11), 1, (11, 14), 2, (14, 16))
-LAG = 4
+FIRST = 3
+LAG = 3
+AHEAD = 6
+EARLY = 6
 
 
 def basis_table(count):
@@ -138,13 +139,18 @@
             copy(dsend.at[c, peer, pick], drecv.at[c, deep, pick], peer).start()
         drecv[c, deep, pick] = dsend[c, deep, pick]
 
-    def group_x(first, last):
-        @pl.loop(0, ny)
+    def rest_x(start, stop):
+        @pl.loop(start, stop)
         def _(y):
-            transform_x(y, first, last, vhi[y], vlo[y])
-
-        @pl.loop(first, last)
-        def _(c):
+            transform_x(y, FIRST, chunks, vhi[y], vlo[y])
+
+    def send(c):
+        if not isinstance(c, int):
+            north(c, c, None, True)
+        elif c in (0, chunks - 1):
+            north(c, c, 0, True)
+            north(c, chunks + (c > 0), 1, True)
+        elif c < chunks:
             north(c, c, None, True)
 
     def stage_y(c, slot, tile=None):
@@ -195,55 +201,68 @@
     for copy in loads[1:]:
         copy.start()
     pl.semaphore_wait(barrier, nn - 1 + nd - 1)
-    north(0, 0, 0, True)
-    north(0, chunks, 1, True)
-    for c in range(1, FIRST):
-        north(c, c, None, True)
-
-    done = 1
-    for item in PLAN:
-        if item == "start":
-            for copy in loads[1:]:
-                copy.wait()
-            stage_y(0, 0, 0)
-            stage_y(0, chunks, 1)
-        elif isinstance(item, tuple):
-            group_x(*item)
-        else:
-            stage_y(item, item)
-            done = item + 1
+    for c in range(FIRST):
+        send(c)
+    rest_x(0, EARLY)
+    for copy in loads[1:]:
+        copy.wait()
+    stage_y(0, 0, 0)
+    rest_x(EARLY, EARLY + 1)
+    stage_y(0, chunks, 1)
+    rest_x(EARLY + 1, ny)
+
+    @pl.loop(FIRST, AHEAD)
+    def _(c):
+        send(c)
 
     lane = lax.broadcasted_iota(jnp.int32, (share_y, full_y), 1)
     row = lax.broadcasted_iota(jnp.int32, (share_y, full_y), 0)
     mine = jnp.where(lane == row + deep * share_y, sym_y[...], 0.0)
     syz[...] = jnp.sum(mine, axis=1, keepdims=True) + sym_z[...]
 
-    @pl.loop(done, LAG)
+    @pl.loop(1, LAG)
     def _(c):
         stage_y(c, c)
+        send(c + AHEAD - 1)
 
     vertical(0, 0, 0, False).wait_recv()
     vertical(0, chunks, 1, False).wait_recv()
     stage_y(LAG, LAG)
+    send(LAG + AHEAD - 1)
     stage_z(0)
 
-    @pl.loop(LAG + 1, chunks)
+    @pl.loop(LAG + 1, chunks - AHEAD)
+    def _(c):
+        stage_y(c, c)
+        send(c + AHEAD - 1)
+        vertical(c - LAG, c - LAG, None, False).wait_recv()
+        stage_z(c - LAG)
+
+    send(chunks - 1)
+
+    @pl.loop(chunks - AHEAD, chunks - 1)
     def _(c):
         stage_y(c, c)
         vertical(c - LAG, c - LAG, None, False).wait_recv()
         stage_z(c - LAG)
 
-    @pl.loop(chunks - LAG, chunks)
+    stage_y(chunks - 1, chunks - 1, 0)
+    stage_y(chunks - 1, chunks + 1, 1)
+
+    @pl.loop(chunks - 1 - LAG, chunks - 1)
     def _(c):
         vertical(c, c, None, False).wait_recv()
         stage_z(c)
 
-    north(0, 0, 0, False).wait_send()
-    north(0, chunks, 1, False).wait_send()
-    vertical(0, 0, 0, False).wait_send()
-    vertical(0, chunks, 1, False).wait_send()
-
-    @pl.loop(1, chunks)
+    vertical(chunks - 1, chunks - 1, 0, False).wait_recv()
+    vertical(chunks - 1, chunks + 1, 1, False).wait_recv()
+    stage_z(chunks - 1)
+
+    for c, slot, tile in ((0, 0, 0), (0, chunks, 1), (chunks - 1, chunks - 1, 0), (chunks - 1, chunks + 1, 1)):
+        north(c, slot, tile, False).wait_send()
+        vertical(c, slot, tile, False).wait_send()
+
+    @pl.loop(1, chunks - 1)
     def _(c):
         north(c, c, None, False).wait_send()
         vertical(c, c, None, False).wait_send()
@@ -282,7 +301,7 @@
             pltpu.VMEM((1, full_y), F32),
             pltpu.VMEM((1, full_z), F32),
             dma((ny,)), dma((6,)),
-            dma((CHUNKS + 1,)), dma((CHUNKS + 1,)), dma((CHUNKS + 1,)), dma((CHUNKS + 1,)),
+            dma((CHUNKS + 2,)), dma((CHUNKS + 2,)), dma((CHUNKS + 2,)), dma((CHUNKS + 2,)),
         ],
         compiler_params=pltpu.CompilerParams(
             collective_id=0, has_side_effects=True, vmem_limit_bytes=32 << 20

time: 69.2 us -> 67.7 us (0.978)
  Pallas kernels: 66.9 us -> 65.1 us
    pallas_call x1, Pallas kernels: 66.9 us -> 65.1 us  [on_device(): pl.pallas_call(functools.partial(kernel, nn, nd), out_shape=jax.ShapeDtyp...]
where the time goes in v3:
time: 67.7 us; the launch traced here: 67.1 us
  Pallas kernels  65.1 us (96%)
  local copies, waits for them, and re-layouts  2.02 us (3%)
    pallas_call x1, Pallas kernels, on_device(): pl.pallas_call(functools.partial(kernel, nn, nd), out_shape=jax.ShapeDtyp...  65.1 us
    unnamed x1, local copies, waits for them, and re-layouts  2.02 us

profile of v3, /device:TPU:0, one launch (start us, length us, event | category | flops | bytes accessed | tf_op | source)
XLA Modules:
  0.0 67.1 jit_solution(12449366876432372576)
XLA Ops:
  0.0 65.1 %shard_map.73 = f32[4,16,64,256]{3,2,1,0:T(8,128)S(1)} custom-call(f32[4,8,64,512]{3,2,1,0:T(8,128)} %bitcast.3, bf16[2,512,512]{2,1,0:T(8,128)(2,1)} %constant.4.clone.hx_hbm, bf16[2,256,256]{2,1,0:T(8,128)(2,1)} %constant.5.clone.hy_hbm, f32[4,4]{1,0:T(4,128)} %coupling_hbm.1, f32[512]{0:T(512)} %sym_x_hbm.1, f32[1,256]{1,0:T(1,128)} %bitcast.4, ...), custom_call_target="tpu_custom_call" | custom-call | tf_op jit(solution)/shard_map/pallas_call | solution.py:283
  65.1 2.0 %copy.9 = f32[4,16,64,256]{3,2,1,0:T(8,128)} copy(f32[4,16,64,256]{3,2,1,0:T(8,128)S(1)} %shard_map.73) | data formatting | bytes 8388608

commit v4 on v2

--- a/solution.py
+++ b/solution.py
@@ -11,9 +11,9 @@
 MESH = pl.DeviceIdType.MESH
 F32, BF16 = jnp.float32, jnp.bfloat16
 CHUNKS = 16
-FIRST = 2
-PLAN = ((2, 8), "start", (8, 11), 1, (11, 14), 2, (14, 16))
-LAG = 4
+FIRST = 3
+LAG = 3
+AHEAD = 4
 
 
 def basis_table(count):
@@ -77,10 +77,12 @@
     cores = [lax.rem(me + i, 2) for i in range(2)]
     steps = [(a, b, c) for a in range(4) for b in range(4) for c in range(2)][1:]
     others = [along_y[a] + along_x[b] + cores[c] for a, b, c in steps]
-    above = [lax.rem(deep + i, nd) for i in range(1, nd)]
+    hops = [min(a, 4 - a) + min(b, 4 - b) for a, b, c in steps]
+    farthest = [others[k] for k in sorted(range(len(steps)), key=lambda k: -hops[k])]
+    above = [lax.rem(deep + i, nd) for i in (1, 2, 3)]
 
     barrier = pltpu.get_barrier_semaphore()
-    for peer in others:
+    for peer in farthest:
         pl.semaphore_signal(
             barrier, inc=1, device_id={"north": peer, "deep": deep}, device_id_type=MESH
         )
@@ -98,8 +100,8 @@
             for t in range(tiles):
                 sbuf[c, t, pl.ds(y, span, stride=ny), :] = part[:, t * 128 : (t + 1) * 128]
 
-    def north(c, slot, tile, start):
-        pick = pl.ds(0, tiles) if tile is None else pl.ds(tile, 1)
+    def north(c, t, start):
+        slot = c * tiles + t
 
         def copy(source, target, peer):
             return pltpu.make_async_remote_copy(
@@ -112,14 +114,14 @@
             )
 
         if not start:
-            everything = rbuf.at[c, pick, pl.ds(0, nn - 1)]
+            everything = rbuf.at[c, t, pl.ds(0, nn - 1)]
             return copy(everything, everything, me)
-        for peer in others:
-            copy(sbuf.at[c, pick, pl.ds(pl.multiple_of(peer * piece, piece), piece)], rbuf.at[c, pick, me], peer).start()
-        rbuf[c, pick, me] = sbuf[c, pick, pl.ds(pl.multiple_of(me * piece, piece), piece), :]
-
-    def vertical(c, slot, tile, start):
-        pick = pl.ds(0, tiles) if tile is None else pl.ds(tile, 1)
+        for peer in farthest:
+            copy(sbuf.at[c, t, pl.ds(pl.multiple_of(peer * piece, piece), piece)], rbuf.at[c, t, me], peer).start()
+        rbuf[c, t, me] = sbuf[c, t, pl.ds(pl.multiple_of(me * piece, piece), piece), :]
+
+    def vertical(c, t, start):
+        slot = c * tiles + t
 
         def copy(source, target, peer):
             return pltpu.make_async_remote_copy(
@@ -132,40 +134,35 @@
             )
 
         if not start:
-            everything = drecv.at[c, pl.ds(0, nd - 1), pick]
+            everything = drecv.at[c, t, pl.ds(0, nd - 1)]
             return copy(everything, everything, deep)
         for peer in above:
-            copy(dsend.at[c, peer, pick], drecv.at[c, deep, pick], peer).start()
-        drecv[c, deep, pick] = dsend[c, deep, pick]
-
-    def group_x(first, last):
-        @pl.loop(0, ny)
+            copy(dsend.at[c, t, peer], drecv.at[c, t, deep], peer).start()
+        drecv[c, t, deep] = dsend[c, t, deep]
+
+    def rest_x(start, stop):
+        @pl.loop(start, stop)
         def _(y):
-            transform_x(y, first, last, vhi[y], vlo[y])
-
-        @pl.loop(first, last)
-        def _(c):
-            north(c, c, None, True)
-
-    def stage_y(c, slot, tile=None):
-        north(c, slot, tile, False).wait_recv()
-        span = range(tiles) if tile is None else (tile,)
+            transform_x(y, FIRST, chunks, vhi[y], vlo[y])
+
+    def stage_y(c, t):
+        north(c, t, False).wait_recv()
         for j in range(rows):
-            columns = [rbuf[c, t, :, pl.ds(j * ny, ny), :].reshape(full_y, 128) for t in span]
-            high, low = split(jnp.concatenate(columns, axis=1))
+            high, low = split(rbuf[c, t, :, pl.ds(j * ny, ny), :].reshape(full_y, 128))
             result = product(hy[0], hy[1], high, low)
             for d in range(nd):
-                for k, t in enumerate(span):
-                    dsend[c, d, t, j] = result[d * share_y : (d + 1) * share_y, k * 128 : (k + 1) * 128]
-        vertical(c, slot, tile, True)
+                dsend[c, t, d, j] = result[d * share_y : (d + 1) * share_y]
+        vertical(c, t, True)
 
     lower = lax.broadcasted_iota(jnp.int32, (share_y, 128), 1) < nz
 
     def stage_z(c):
+        for t in range(tiles):
+            vertical(c, t, False).wait_recv()
         for j in range(rows):
             lines = []
             for t in range(tiles):
-                parts = [drecv[c, d, t, j] for d in range(nd)]
+                parts = [drecv[c, t, d, j] for d in range(nd)]
                 turned = [pltpu.roll(p, nz, 1) for p in parts]
                 even = [jnp.where(lower, parts[d], turned[d + 1]) for d in range(0, nd, 2)]
                 odd = [jnp.where(lower, turned[d], parts[d + 1]) for d in range(0, nd, 2)]
@@ -195,58 +192,57 @@
     for copy in loads[1:]:
         copy.start()
     pl.semaphore_wait(barrier, nn - 1 + nd - 1)
-    north(0, 0, 0, True)
-    north(0, chunks, 1, True)
-    for c in range(1, FIRST):
-        north(c, c, None, True)
-
-    done = 1
-    for item in PLAN:
-        if item == "start":
-            for copy in loads[1:]:
-                copy.wait()
-            stage_y(0, 0, 0)
-            stage_y(0, chunks, 1)
-        elif isinstance(item, tuple):
-            group_x(*item)
-        else:
-            stage_y(item, item)
-            done = item + 1
+    north(0, 0, True)
+    rest_x(0, 2)
+    north(0, 1, True)
+    rest_x(2, 4)
+    north(1, 0, True)
+    north(1, 1, True)
+    rest_x(4, 7)
+    for copy in loads[1:]:
+        copy.wait()
+    stage_y(0, 0)
+    north(2, 0, True)
+    north(2, 1, True)
+    stage_y(0, 1)
+    rest_x(7, 8)
+    for c in range(FIRST, AHEAD):
+        for t in range(tiles):
+            north(c, t, True)
 
     lane = lax.broadcasted_iota(jnp.int32, (share_y, full_y), 1)
     row = lax.broadcasted_iota(jnp.int32, (share_y, full_y), 0)
     mine = jnp.where(lane == row + deep * share_y, sym_y[...], 0.0)
     syz[...] = jnp.sum(mine, axis=1, keepdims=True) + sym_z[...]
 
-    @pl.loop(done, LAG)
-    def _(c):
-        stage_y(c, c)
-
-    vertical(0, 0, 0, False).wait_recv()
-    vertical(0, chunks, 1, False).wait_recv()
-    stage_y(LAG, LAG)
-    stage_z(0)
-
-    @pl.loop(LAG + 1, chunks)
-    def _(c):
-        stage_y(c, c)
-        vertical(c - LAG, c - LAG, None, False).wait_recv()
-        stage_z(c - LAG)
+    def step(c, more, ready):
+        stage_y(c, 0)
+        if more:
+            north(c + AHEAD - 1, 0, True)
+        if ready:
+            stage_z(c - LAG)
+        stage_y(c, 1)
+        if more:
+            north(c + AHEAD - 1, 1, True)
+
+    for first, last, more, ready in (
+        (1, LAG, True, False),
+        (LAG, chunks - AHEAD + 1, True, True),
+        (chunks - AHEAD + 1, chunks, False, True),
+    ):
+        @pl.loop(first, last)
+        def _(c):
+            step(c, more, ready)
 
     @pl.loop(chunks - LAG, chunks)
     def _(c):
-        vertical(c, c, None, False).wait_recv()
         stage_z(c)
 
-    north(0, 0, 0, False).wait_send()
-    north(0, chunks, 1, False).wait_send()
-    vertical(0, 0, 0, False).wait_send()
-    vertical(0, chunks, 1, False).wait_send()
-
-    @pl.loop(1, chunks)
+    @pl.loop(0, chunks)
     def _(c):
-        north(c, c, None, False).wait_send()
-        vertical(c, c, None, False).wait_send()
+        for t in range(tiles):
+            north(c, t, False).wait_send()
+            vertical(c, t, False).wait_send()
 
 
 def on_device(nn, nd, velocity, coupling, symbol_x, symbol_y, symbol_z):
@@ -274,15 +270,15 @@
             pltpu.VMEM((2, full_y, full_y), BF16),
             pltpu.VMEM((CHUNKS, tiles, nn * rows * ny, 128), F32),
             pltpu.VMEM((CHUNKS, tiles, nn, rows * ny, 128), F32),
-            pltpu.VMEM((CHUNKS, nd, tiles, rows, share_y, 128), F32),
-            pltpu.VMEM((CHUNKS, nd, tiles, rows, share_y, 128), F32),
+            pltpu.VMEM((CHUNKS, tiles, nd, rows, share_y, 128), F32),
+            pltpu.VMEM((CHUNKS, tiles, nd, rows, share_y, 128), F32),
             pltpu.VMEM((share_y, full_z), F32),
             pltpu.SMEM((fields, fields), F32),
             pltpu.SMEM((nx,), F32),
             pltpu.VMEM((1, full_y), F32),
             pltpu.VMEM((1, full_z), F32),
             dma((ny,)), dma((6,)),
-            dma((CHUNKS + 1,)), dma((CHUNKS + 1,)), dma((CHUNKS + 1,)), dma((CHUNKS + 1,)),
+            dma((CHUNKS * tiles,)), dma((CHUNKS * tiles,)), dma((CHUNKS * tiles,)), dma((CHUNKS * tiles,)),
         ],
         compiler_params=pltpu.CompilerParams(
             collective_id=0, has_side_effects=True, vmem_limit_bytes=32 << 20

time: 69.2 us -> 66.3 us (0.958)
  Pallas kernels: 66.9 us -> 63.9 us
    pallas_call x1, Pallas kernels: 66.9 us -> 63.9 us  [on_device(): pl.pallas_call(functools.partial(kernel, nn, nd), out_shape=jax.ShapeDtyp...]
where the time goes in v4:
time: 66.3 us; the launch traced here: 65.9 us
  Pallas kernels  63.9 us (96%)
  local copies, waits for them, and re-layouts  2.02 us (3%)
    pallas_call x1, Pallas kernels, on_device(): pl.pallas_call(functools.partial(kernel, nn, nd), out_shape=jax.ShapeDtyp...  63.9 us
    unnamed x1, local copies, waits for them, and re-layouts  2.02 us

profile of v4, /device:TPU:0, one launch (start us, length us, event | category | flops | bytes accessed | tf_op | source)
XLA Modules:
  0.0 65.9 jit_solution(16180445967993933666)
XLA Ops:
  0.0 63.9 %shard_map.73 = f32[4,16,64,256]{3,2,1,0:T(8,128)S(1)} custom-call(f32[4,8,64,512]{3,2,1,0:T(8,128)} %bitcast.3, bf16[2,512,512]{2,1,0:T(8,128)(2,1)} %constant.4.clone.hx_hbm, bf16[2,256,256]{2,1,0:T(8,128)(2,1)} %constant.5.clone.hy_hbm, f32[4,4]{1,0:T(4,128)} %coupling_hbm.1, f32[512]{0:T(512)} %sym_x_hbm.1, f32[1,256]{1,0:T(1,128)} %bitcast.4, ...), custom_call_target="tpu_custom_call" | custom-call | tf_op jit(solution)/shard_map/pallas_call | solution.py:260
  63.9 2.0 %copy.9 = f32[4,16,64,256]{3,2,1,0:T(8,128)} copy(f32[4,16,64,256]{3,2,1,0:T(8,128)S(1)} %shard_map.73) | data formatting | bytes 8388608

commit v5 on v4

--- a/solution.py
+++ b/solution.py
@@ -44,8 +44,55 @@
     return both[:count] + (both[count:] + dot(a_high, b_low, transposed))
 
 
+def transform_z(pieces, table, nz):
+    lower = lax.broadcasted_iota(jnp.int32, pieces[0][0].shape, 1) < nz
+    lines = []
+    for parts in pieces:
+        turned = [pltpu.roll(p, nz, 1) for p in parts]
+        pairs = range(0, len(parts), 2)
+        even = [jnp.where(lower, parts[d], turned[d + 1]) for d in pairs]
+        odd = [jnp.where(lower, turned[d], parts[d + 1]) for d in pairs]
+        lines.append(jnp.concatenate(even, axis=1))
+        lines.append(jnp.concatenate(odd, axis=1))
+    high, low = split(jnp.concatenate(lines, axis=0))
+    result = product(high, low, table[0], table[1])
+    share = pieces[0][0].shape[0]
+    return [result[f * share : (f + 1) * share] for f in range(len(lines))]
+
+
+def mixed_with(old, coupling, weight):
+    rest = 1.0 - weight
+    for a in range(len(old)):
+        mixed = coupling(a, 0) * old[0]
+        for b in range(1, len(old)):
+            mixed = mixed + coupling(a, b) * old[b]
+        yield weight * old[a] + rest * mixed
+
+
+def finish(nz, most, last, table, weight, coupling, result, final, sem):
+    fields, share_x = most.shape[:2]
+    copies = [
+        pltpu.make_async_copy(most.at[f, pl.ds(0, share_x - 1)], result.at[f, pl.ds(0, share_x - 1)], sem.at[f])
+        for f in range(fields)
+    ]
+    for copy in copies:
+        copy.start()
+    tiles, nd = last.shape[:2]
+    old = transform_z([[last[t, d] for d in range(nd)] for t in range(tiles)], table, nz)
+
+    def factor(a, b):
+        return coupling[pl.ds(a * fields + b, 1), :]
+
+    for a, values in enumerate(mixed_with(old, factor, weight[...])):
+        final[a] = values
+        copies.append(pltpu.make_async_copy(final.at[a], result.at[a, share_x - 1], sem.at[fields + a]))
+        copies[-1].start()
+    for copy in copies:
+        copy.wait()
+
+
 def kernel(
-    nn, nd, v_hbm, hx_hbm, hy_hbm, coupling_hbm, sym_x_hbm, sym_y_hbm, sym_z_hbm, out,
+    nn, nd, v_hbm, hx_hbm, hy_hbm, coupling_hbm, sym_x_hbm, sym_y_hbm, sym_z_hbm, out, tail, table, weight, mixing,
     vbuf, vhi, vlo, hx, hy, sbuf, rbuf, dsend, drecv, syz, coupling, sym_x, sym_y, sym_z,
     vsem, hsem, ssem, rsem, dssem, drsem,
 ):
@@ -60,16 +107,25 @@
     piece = rows * ny
     me, deep = lax.axis_index("north"), lax.axis_index("deep")
 
+    soon = FIRST * nn * rows
     loads = [
         pltpu.make_async_copy(a, b, hsem.at[k])
         for k, (a, b) in enumerate((
-            (hx_hbm, hx), (hy_hbm, hy), (coupling_hbm, coupling), (sym_x_hbm, sym_x),
+            (hx_hbm.at[:, pl.ds(0, soon)], hx.at[:, pl.ds(0, soon)]),
+            (hx_hbm.at[:, pl.ds(soon, nx - soon)], hx.at[:, pl.ds(soon, nx - soon)]), (hy_hbm, hy), (coupling_hbm, coupling), (sym_x_hbm, sym_x),
             (sym_y_hbm, sym_y), (sym_z_hbm, sym_z),
         ))
     ]
-    load_v = [pltpu.make_async_copy(v_hbm.at[:, y], vbuf.at[y], vsem.at[y]) for y in range(ny)]
+    per = fields // tiles
+    load_v = [
+        [
+            pltpu.make_async_copy(v_hbm.at[pl.ds(t * per, per), y], vbuf.at[y, pl.ds(t * per, per)], vsem.at[t, y])
+            for y in range(ny)
+        ]
+        for t in range(tiles)
+    ]
     loads[0].start()
-    for copy in load_v:
+    for copy in load_v[0] + load_v[1] + loads[1:2]:
         copy.start()
 
     along_y = [lax.rem(me // 8 + i, 4) * 8 for i in range(4)]
@@ -91,14 +147,24 @@
             barrier, inc=1, device_id={"north": me, "deep": peer}, device_id_type=MESH
         )
 
-    def transform_x(y, first, last, high, low):
+    def transform_x(y, first, last, high, low, begin):
         span = nn * rows
         pick = pl.ds(first * span, (last - first) * span)
         result = product(hx[0, pick, :], hx[1, pick, :], high, low, transposed=True)
         for c in range(first, last):
             part = result[(c - first) * span : (c - first + 1) * span]
-            for t in range(tiles):
-                sbuf[c, t, pl.ds(y, span, stride=ny), :] = part[:, t * 128 : (t + 1) * 128]
+            for k in range(part.shape[1] // 128):
+                sbuf[c, begin + k, pl.ds(y, span, stride=ny), :] = part[:, k * 128 : (k + 1) * 128]
+
+    def first_x(t):
+        for y in range(0, ny, 2):
+            load_v[t][y].wait()
+            load_v[t][y + 1].wait()
+            for k in (y, y + 1):
+                high, low = split(vbuf[k, t * per : (t + 1) * per].reshape(128, nx))
+                vhi[k, t * 128 : (t + 1) * 128] = high
+                vlo[k, t * 128 : (t + 1) * 128] = low
+                transform_x(k, 0, FIRST, high, low, t)
 
     def north(c, t, start):
         slot = c * tiles + t
@@ -143,7 +209,7 @@
     def rest_x(start, stop):
         @pl.loop(start, stop)
         def _(y):
-            transform_x(y, FIRST, chunks, vhi[y], vlo[y])
+            transform_x(y, FIRST, chunks, vhi[y], vlo[y], 0)
 
     def stage_y(c, t):
         north(c, t, False).wait_recv()
@@ -154,58 +220,39 @@
                 dsend[c, t, d, j] = result[d * share_y : (d + 1) * share_y]
         vertical(c, t, True)
 
-    lower = lax.broadcasted_iota(jnp.int32, (share_y, 128), 1) < nz
+    def weight_of(x):
+        return 1.0 / (1.0 + (sym_x[me * share_x + x] + syz[...]))
 
     def stage_z(c):
         for t in range(tiles):
             vertical(c, t, False).wait_recv()
         for j in range(rows):
-            lines = []
-            for t in range(tiles):
-                parts = [drecv[c, t, d, j] for d in range(nd)]
-                turned = [pltpu.roll(p, nz, 1) for p in parts]
-                even = [jnp.where(lower, parts[d], turned[d + 1]) for d in range(0, nd, 2)]
-                odd = [jnp.where(lower, turned[d], parts[d + 1]) for d in range(0, nd, 2)]
-                lines.append(jnp.concatenate(even, axis=1))
-                lines.append(jnp.concatenate(odd, axis=1))
-            high, low = split(jnp.concatenate(lines, axis=0))
-            result = product(high, low, hy[0], hy[1])
-            old = [result[f * share_y : (f + 1) * share_y] for f in range(fields)]
             x = c * rows + j
-            weight = 1.0 / (1.0 + (sym_x[me * share_x + x] + syz[...]))
-            rest = 1.0 - weight
-            for a in range(fields):
-                mixed = coupling[a, 0] * old[0]
-                for b in range(1, fields):
-                    mixed = mixed + coupling[a, b] * old[b]
-                out[a, x] = weight * old[a] + rest * mixed
+            old = transform_z([[drecv[c, t, d, j] for d in range(nd)] for t in range(tiles)], hy, nz)
+            for a, values in enumerate(mixed_with(old, lambda a, b: coupling[a, b], weight_of(x))):
+                out[a, x] = values
 
     loads[0].wait()
-    for y in range(0, ny, 2):
-        load_v[y].wait()
-        load_v[y + 1].wait()
-        for k in (y, y + 1):
-            high, low = split(vbuf[k].reshape(wide, nx))
-            vhi[k] = high
-            vlo[k] = low
-            transform_x(k, 0, FIRST, high, low)
-    for copy in loads[1:]:
+    first_x(0)
+    for copy in loads[2:]:
         copy.start()
     pl.semaphore_wait(barrier, nn - 1 + nd - 1)
     north(0, 0, True)
+    first_x(1)
+    north(0, 1, True)
+    loads[1].wait()
     rest_x(0, 2)
-    north(0, 1, True)
-    rest_x(2, 4)
     north(1, 0, True)
     north(1, 1, True)
-    rest_x(4, 7)
-    for copy in loads[1:]:
+    rest_x(2, 5)
+    for copy in loads[2:]:
         copy.wait()
     stage_y(0, 0)
     north(2, 0, True)
+    rest_x(5, 6)
+    stage_y(0, 1)
     north(2, 1, True)
-    stage_y(0, 1)
-    rest_x(7, 8)
+    rest_x(6, 8)
     for c in range(FIRST, AHEAD):
         for t in range(tiles):
             north(c, t, True)
@@ -234,9 +281,19 @@
         def _(c):
             step(c, more, ready)
 
-    @pl.loop(chunks - LAG, chunks)
+    @pl.loop(chunks - LAG, chunks - 1)
     def _(c):
         stage_z(c)
+
+    table[...] = hy[...]
+    weight[...] = weight_of(share_x - 1)
+    for a in range(fields):
+        for b in range(fields):
+            mixing[pl.ds(a * fields + b, 1), :] = jnp.full((1, mixing.shape[1]), coupling[a, b], F32)
+    for t in range(tiles):
+        vertical(chunks - 1, t, False).wait_recv()
+        for d in range(nd):
+            tail[t, d] = drecv[chunks - 1, t, d, 0]
 
     @pl.loop(0, chunks)
     def _(c):
@@ -257,11 +314,18 @@
     table_x = jnp.asarray(two_parts(basis_table(nx)[order]))
     table_y = jnp.asarray(two_parts(basis_table(full_y)))
     dma = pltpu.SemaphoreType.DMA
-    return pl.pallas_call(
+    vector = pl.BlockSpec(memory_space=pltpu.VMEM)
+    made = pl.pallas_call(
         functools.partial(kernel, nn, nd),
-        out_shape=jax.ShapeDtypeStruct((fields, share_x, share_y, full_z), F32),
+        out_shape=(
+            jax.ShapeDtypeStruct((fields, share_x, share_y, full_z), F32),
+            jax.ShapeDtypeStruct((tiles, nd, share_y, 128), F32),
+            jax.ShapeDtypeStruct((2, full_y, full_y), BF16),
+            jax.ShapeDtypeStruct((share_y, full_z), F32),
+            jax.ShapeDtypeStruct((fields * fields, full_z), F32),
+        ),
         in_specs=[pl.BlockSpec(memory_space=pltpu.MemorySpace.HBM)] * 7,
-        out_specs=pl.BlockSpec(memory_space=pltpu.VMEM),
+        out_specs=(vector,) * 5,
         scratch_shapes=[
             pltpu.VMEM((ny, fields, nz, nx), F32),
             pltpu.VMEM((ny, wide, nx), BF16),
@@ -277,7 +341,7 @@
             pltpu.SMEM((nx,), F32),
             pltpu.VMEM((1, full_y), F32),
             pltpu.VMEM((1, full_z), F32),
-            dma((ny,)), dma((6,)),
+            dma((tiles, ny)), dma((7,)),
             dma((CHUNKS * tiles,)), dma((CHUNKS * tiles,)), dma((CHUNKS * tiles,)), dma((CHUNKS * tiles,)),
         ],
         compiler_params=pltpu.CompilerParams(
@@ -291,6 +355,15 @@
         )
     ))
 
+    return pl.pallas_call(
+        functools.partial(finish, nz),
+        out_shape=jax.ShapeDtypeStruct((fields, share_x, share_y, full_z), F32),
+        in_specs=[vector] * 5,
+        out_specs=pl.BlockSpec(memory_space=pl.ANY),
+        scratch_shapes=[pltpu.VMEM((fields, share_y, full_z), F32), dma((2 * fields,))],
+        compiler_params=pltpu.CompilerParams(vmem_limit_bytes=8 << 20),
+    )(*made)
+
 
 def solution(mesh):
     placed = (P(None, None, "north", "deep"), P(), P(), P(), P())

time: 66.3 us -> 66 us (level)
  local copies, waits for them, and re-layouts: 2.02 us -> 0 us
  Pallas kernels: 63.9 us -> 65.6 us
    unnamed x1 -> x0, local copies, waits for them, and re-layouts: 2.02 us -> none
    pallas_call x1 -> x2, Pallas kernels: 63.9 us -> 65.6 us  [the longest x1 63.5 us: on_device(): pl.pallas_call(functools.partial(kernel, nn, nd), out_shape=(jax.ShapeDty...]
where the time goes in v5:
time: 66 us; the launch traced here: 65.6 us
  Pallas kernels  65.6 us (99%)
    pallas_call x1, Pallas kernels, on_device(): pl.pallas_call(functools.partial(kernel, nn, nd), out_shape=(jax.ShapeDty...  63.5 us
    pallas_call x1, Pallas kernels, on_device(): pl.pallas_call(functools.partial(finish, nz), out_shape=jax.ShapeDtypeStr...  2.06 us

profile of v5, /device:TPU:0, one launch (start us, length us, event | category | flops | bytes accessed | tf_op | source)
XLA Modules:
  0.0 65.6 jit_solution(3930220708593040087)
XLA Ops:
  0.0 63.5 %shard_map.73 = (f32[4,16,64,256]{3,2,1,0:T(8,128)S(1)}, f32[2,4,64,128]{3,2,1,0:T(8,128)S(1)}, bf16[2,256,256]{2,1,0:T(8,128)(2,1)S(1)}, f32[64,256]{1,0:T(8,128)S(1)}, f32[16,256]{1,0:T(8,128)S(1)}) custom-call(f32[4,8,64,512]{3,2,1,0:T(8,128)} %bitcast.3, bf16[2,512,512]{2,1,0:T(8,128)(2,1)} %constant.4.clone.hx_hbm, ...), custom_call_target="tpu_custom_call" | custom-call | tf_op jit(solution)/shard_map/pallas_call | solution.py:318
  63.5 2.1 %shard_map.74 = f32[4,16,64,256]{3,2,1,0:T(8,128)} custom-call(f32[4,16,64,256]{3,2,1,0:T(8,128)S(1)} %get-tuple-element.10.most, f32[2,4,64,128]{3,2,1,0:T(8,128)S(1)} %get-tuple-element.11.last, bf16[2,256,256]{2,1,0:T(8,128)(2,1)S(1)} %get-tuple-element.12.table, f32[64,256]{1,0:T(8,128)S(1)} %get-tuple-element.13.weight, ...), custom_call_target="tpu_custom_call" | custom-call | tf_op jit(solution)/shard_map/pallas_call | solution.py:358

commit v6 on v5

--- a/solution.py
+++ b/solution.py
@@ -119,8 +119,10 @@
     per = fields // tiles
     load_v = [
         [
-            pltpu.make_async_copy(v_hbm.at[pl.ds(t * per, per), y], vbuf.at[y, pl.ds(t * per, per)], vsem.at[t, y])
-            for y in range(ny)
+            pltpu.make_async_copy(
+                v_hbm.at[pl.ds(t * per, per), pl.ds(y, 2)], vbuf.at[pl.ds(t * per, per), pl.ds(y, 2)], vsem.at[t, y // 2]
+            )
+            for y in range(0, ny, 2)
         ]
         for t in range(tiles)
     ]
@@ -158,10 +160,9 @@
 
     def first_x(t):
         for y in range(0, ny, 2):
-            load_v[t][y].wait()
-            load_v[t][y + 1].wait()
+            load_v[t][y // 2].wait()
             for k in (y, y + 1):
-                high, low = split(vbuf[k, t * per : (t + 1) * per].reshape(128, nx))
+                high, low = split(vbuf[t * per : (t + 1) * per, k].reshape(128, nx))
                 vhi[k, t * 128 : (t + 1) * 128] = high
                 vlo[k, t * 128 : (t + 1) * 128] = low
                 transform_x(k, 0, FIRST, high, low, t)
@@ -173,7 +174,7 @@
             return pltpu.make_async_remote_copy(
                 src_ref=source,
                 dst_ref=target,
-                send_sem=ssem.at[slot],
+                send_sem=ssem.at[0],
                 recv_sem=rsem.at[slot],
                 device_id={"north": peer, "deep": deep},
                 device_id_type=MESH,
@@ -193,7 +194,7 @@
             return pltpu.make_async_remote_copy(
                 src_ref=source,
                 dst_ref=target,
-                send_sem=dssem.at[slot],
+                send_sem=dssem.at[0],
                 recv_sem=drsem.at[slot],
                 device_id={"north": me, "deep": peer},
                 device_id_type=MESH,
@@ -295,11 +296,16 @@
         for d in range(nd):
             tail[t, d] = drecv[chunks - 1, t, d, 0]
 
-    @pl.loop(0, chunks)
-    def _(c):
-        for t in range(tiles):
-            north(c, t, False).wait_send()
-            vertical(c, t, False).wait_send()
+    for buffer, count, sent, received in ((rbuf, nn - 1, ssem, rsem), (drecv, nd - 1, dssem, drsem)):
+        everything = buffer.at[:, :, pl.ds(0, count)]
+        pltpu.make_async_remote_copy(
+            src_ref=everything,
+            dst_ref=everything,
+            send_sem=sent.at[0],
+            recv_sem=received.at[0],
+            device_id={"north": me, "deep": deep},
+            device_id_type=MESH,
+        ).wait_send()
 
 
 def on_device(nn, nd, velocity, coupling, symbol_x, symbol_y, symbol_z):
@@ -327,7 +333,7 @@
         in_specs=[pl.BlockSpec(memory_space=pltpu.MemorySpace.HBM)] * 7,
         out_specs=(vector,) * 5,
         scratch_shapes=[
-            pltpu.VMEM((ny, fields, nz, nx), F32),
+            pltpu.VMEM((fields, ny, nz, nx), F32),
             pltpu.VMEM((ny, wide, nx), BF16),
             pltpu.VMEM((ny, wide, nx), BF16),
             pltpu.VMEM((2, nx, nx), BF16),
@@ -341,8 +347,8 @@
             pltpu.SMEM((nx,), F32),
             pltpu.VMEM((1, full_y), F32),
             pltpu.VMEM((1, full_z), F32),
-            dma((tiles, ny)), dma((7,)),
-            dma((CHUNKS * tiles,)), dma((CHUNKS * tiles,)), dma((CHUNKS * tiles,)), dma((CHUNKS * tiles,)),
+            dma((tiles, ny // 2)), dma((7,)),
+            dma((1,)), dma((CHUNKS * tiles,)), dma((1,)), dma((CHUNKS * tiles,)),
         ],
         compiler_params=pltpu.CompilerParams(
             collective_id=0, has_side_effects=True, vmem_limit_bytes=32 << 20

time: 66 us -> 65.1 us (0.986)
  Pallas kernels: 65.6 us -> 64.6 us
    pallas_call x1, Pallas kernels: 63.5 us -> 62.6 us  [on_device(): pl.pallas_call(functools.partial(kernel, nn, nd), out_shape=(jax.ShapeDty...]
where the time goes in v6:
time: 65.1 us; the launch traced here: 64.6 us
  Pallas kernels  64.6 us (99%)
    pallas_call x1, Pallas kernels, on_device(): pl.pallas_call(functools.partial(kernel, nn, nd), out_shape=(jax.ShapeDty...  62.6 us
    pallas_call x1, Pallas kernels, on_device(): pl.pallas_call(functools.partial(finish, nz), out_shape=jax.ShapeDtypeStr...  2.06 us

profile of v6, /device:TPU:0, one launch (start us, length us, event | category | flops | bytes accessed | tf_op | source)
XLA Modules:
  0.0 64.6 jit_solution(2934983799361657591)
XLA Ops:
  0.0 62.6 %shard_map.73 = (f32[4,16,64,256]{3,2,1,0:T(8,128)S(1)}, f32[2,4,64,128]{3,2,1,0:T(8,128)S(1)}, bf16[2,256,256]{2,1,0:T(8,128)(2,1)S(1)}, f32[64,256]{1,0:T(8,128)S(1)}, f32[16,256]{1,0:T(8,128)S(1)}) custom-call(f32[4,8,64,512]{3,2,1,0:T(8,128)} %bitcast.3, bf16[2,512,512]{2,1,0:T(8,128)(2,1)} %constant.4.clone.hx_hbm, ...), custom_call_target="tpu_custom_call" | custom-call | tf_op jit(solution)/shard_map/pallas_call | solution.py:324
  62.6 2.1 %shard_map.74 = f32[4,16,64,256]{3,2,1,0:T(8,128)} custom-call(f32[4,16,64,256]{3,2,1,0:T(8,128)S(1)} %get-tuple-element.10.most, f32[2,4,64,128]{3,2,1,0:T(8,128)S(1)} %get-tuple-element.11.last, bf16[2,256,256]{2,1,0:T(8,128)(2,1)S(1)} %get-tuple-element.12.table, f32[64,256]{1,0:T(8,128)S(1)} %get-tuple-element.13.weight, ...), custom_call_target="tpu_custom_call" | custom-call | tf_op jit(solution)/shard_map/pallas_call | solution.py:364

commit v7 on v6

--- a/solution.py
+++ b/solution.py
@@ -14,6 +14,7 @@
 FIRST = 3
 LAG = 3
 AHEAD = 4
+CYCLE = 8
 
 
 def basis_table(count):
@@ -127,7 +128,7 @@
         for t in range(tiles)
     ]
     loads[0].start()
-    for copy in load_v[0] + load_v[1] + loads[1:2]:
+    for copy in load_v[0]:
         copy.start()
 
     along_y = [lax.rem(me // 8 + i, 4) * 8 for i in range(4)]
@@ -137,7 +138,7 @@
     others = [along_y[a] + along_x[b] + cores[c] for a, b, c in steps]
     hops = [min(a, 4 - a) + min(b, 4 - b) for a, b, c in steps]
     farthest = [others[k] for k in sorted(range(len(steps)), key=lambda k: -hops[k])]
-    above = [lax.rem(deep + i, nd) for i in (1, 2, 3)]
+    above = [k + lax.div(k + nd - deep, nd) for k in range(nd - 1)]
 
     barrier = pltpu.get_barrier_semaphore()
     for peer in farthest:
@@ -149,6 +150,9 @@
             barrier, inc=1, device_id={"north": me, "deep": peer}, device_id_type=MESH
         )
 
+    for copy in load_v[1] + loads[1:2]:
+        copy.start()
+
     def transform_x(y, first, last, high, low, begin):
         span = nn * rows
         pick = pl.ds(first * span, (last - first) * span)
@@ -168,7 +172,7 @@
                 transform_x(k, 0, FIRST, high, low, t)
 
     def north(c, t, start):
-        slot = c * tiles + t
+        slot = c % CYCLE * tiles + t if isinstance(c, int) else lax.rem(c, CYCLE) * tiles + t
 
         def copy(source, target, peer):
             return pltpu.make_async_remote_copy(
@@ -188,7 +192,7 @@
         rbuf[c, t, me] = sbuf[c, t, pl.ds(pl.multiple_of(me * piece, piece), piece), :]
 
     def vertical(c, t, start):
-        slot = c * tiles + t
+        slot = c % CYCLE * tiles + t if isinstance(c, int) else lax.rem(c, CYCLE) * tiles + t
 
         def copy(source, target, peer):
             return pltpu.make_async_remote_copy(
@@ -348,7 +352,7 @@
             pltpu.VMEM((1, full_y), F32),
             pltpu.VMEM((1, full_z), F32),
             dma((tiles, ny // 2)), dma((7,)),
-            dma((1,)), dma((CHUNKS * tiles,)), dma((1,)), dma((CHUNKS * tiles,)),
+            dma((1,)), dma((CYCLE * tiles,)), dma((1,)), dma((CYCLE * tiles,)),
         ],
         compiler_params=pltpu.CompilerParams(
             collective_id=0, has_side_effects=True, vmem_limit_bytes=32 << 20

time: 65.1 us -> 64.7 us (level)
  Pallas kernels: 64.6 us -> 63.9 us
    pallas_call x1, Pallas kernels: 62.6 us -> 61.9 us  [on_device(): pl.pallas_call(functools.partial(kernel, nn, nd), out_shape=(jax.ShapeDty...]
where the time goes in v7:
time: 64.7 us; the launch traced here: 63.9 us
  Pallas kernels  63.9 us (99%)
    pallas_call x1, Pallas kernels, on_device(): pl.pallas_call(functools.partial(kernel, nn, nd), out_shape=(jax.ShapeDty...  61.9 us
    pallas_call x1, Pallas kernels, on_device(): pl.pallas_call(functools.partial(finish, nz), out_shape=jax.ShapeDtypeStr...  2.06 us

profile of v7, /device:TPU:0, one launch (start us, length us, event | category | flops | bytes accessed | tf_op | source)
XLA Modules:
  0.0 63.9 jit_solution(5881041263451172335)
XLA Ops:
  0.0 61.9 %shard_map.73 = (f32[4,16,64,256]{3,2,1,0:T(8,128)S(1)}, f32[2,4,64,128]{3,2,1,0:T(8,128)S(1)}, bf16[2,256,256]{2,1,0:T(8,128)(2,1)S(1)}, f32[64,256]{1,0:T(8,128)S(1)}, f32[16,256]{1,0:T(8,128)S(1)}) custom-call(f32[4,8,64,512]{3,2,1,0:T(8,128)} %bitcast.3, bf16[2,512,512]{2,1,0:T(8,128)(2,1)} %constant.4.clone.hx_hbm, ...), custom_call_target="tpu_custom_call" | custom-call | tf_op jit(solution)/shard_map/pallas_call | solution.py:328
  61.9 2.1 %shard_map.74 = f32[4,16,64,256]{3,2,1,0:T(8,128)} custom-call(f32[4,16,64,256]{3,2,1,0:T(8,128)S(1)} %get-tuple-element.10.most, f32[2,4,64,128]{3,2,1,0:T(8,128)S(1)} %get-tuple-element.11.last, bf16[2,256,256]{2,1,0:T(8,128)(2,1)S(1)} %get-tuple-element.12.table, f32[64,256]{1,0:T(8,128)S(1)} %get-tuple-element.13.weight, ...), custom_call_target="tpu_custom_call" | custom-call | tf_op jit(solution)/shard_map/pallas_call | solution.py:368

commit v8 on v7

--- a/solution.py
+++ b/solution.py
@@ -249,12 +249,12 @@
     rest_x(0, 2)
     north(1, 0, True)
     north(1, 1, True)
-    rest_x(2, 5)
+    rest_x(2, 4)
     for copy in loads[2:]:
         copy.wait()
     stage_y(0, 0)
     north(2, 0, True)
-    rest_x(5, 6)
+    rest_x(4, 6)
     stage_y(0, 1)
     north(2, 1, True)
     rest_x(6, 8)

time: 64.7 us -> 64.2 us (level)
  no operation moved by 1% of the time
where the time goes in v8:
time: 64.2 us; the launch traced here: 63.7 us
  Pallas kernels  63.7 us (99%)
    pallas_call x1, Pallas kernels, on_device(): pl.pallas_call(functools.partial(kernel, nn, nd), out_shape=(jax.ShapeDty...  61.7 us
    pallas_call x1, Pallas kernels, on_device(): pl.pallas_call(functools.partial(finish, nz), out_shape=jax.ShapeDtypeStr...  2.06 us

profile of v8, /device:TPU:0, one launch (start us, length us, event | category | flops | bytes accessed | tf_op | source)
XLA Modules:
  0.0 63.7 jit_solution(6835746769795879178)
XLA Ops:
  0.0 61.7 %shard_map.73 = (f32[4,16,64,256]{3,2,1,0:T(8,128)S(1)}, f32[2,4,64,128]{3,2,1,0:T(8,128)S(1)}, bf16[2,256,256]{2,1,0:T(8,128)(2,1)S(1)}, f32[64,256]{1,0:T(8,128)S(1)}, f32[16,256]{1,0:T(8,128)S(1)}) custom-call(f32[4,8,64,512]{3,2,1,0:T(8,128)} %bitcast.3, bf16[2,512,512]{2,1,0:T(8,128)(2,1)} %constant.4.clone.hx_hbm, ...), custom_call_target="tpu_custom_call" | custom-call | tf_op jit(solution)/shard_map/pallas_call | solution.py:328
  61.7 2.1 %shard_map.74 = f32[4,16,64,256]{3,2,1,0:T(8,128)} custom-call(f32[4,16,64,256]{3,2,1,0:T(8,128)S(1)} %get-tuple-element.10.most, f32[2,4,64,128]{3,2,1,0:T(8,128)S(1)} %get-tuple-element.11.last, bf16[2,256,256]{2,1,0:T(8,128)(2,1)S(1)} %get-tuple-element.12.table, f32[64,256]{1,0:T(8,128)S(1)} %get-tuple-element.13.weight, ...), custom_call_target="tpu_custom_call" | custom-call | tf_op jit(solution)/shard_map/pallas_call | solution.py:368

commit v9 on v8

--- a/solution.py
+++ b/solution.py
@@ -86,8 +86,8 @@
 
     for a, values in enumerate(mixed_with(old, factor, weight[...])):
         final[a] = values
-        copies.append(pltpu.make_async_copy(final.at[a], result.at[a, share_x - 1], sem.at[fields + a]))
-        copies[-1].start()
+    copies.append(pltpu.make_async_copy(final, result.at[:, share_x - 1], sem.at[fields]))
+    copies[-1].start()
     for copy in copies:
         copy.wait()
 
@@ -121,9 +121,9 @@
     load_v = [
         [
             pltpu.make_async_copy(
-                v_hbm.at[pl.ds(t * per, per), pl.ds(y, 2)], vbuf.at[pl.ds(t * per, per), pl.ds(y, 2)], vsem.at[t, y // 2]
+                v_hbm.at[pl.ds(t * per, per), pl.ds(y, 4)], vbuf.at[pl.ds(t * per, per), pl.ds(y, 4)], vsem.at[t, y // 4]
             )
-            for y in range(0, ny, 2)
+            for y in range(0, ny, 4)
         ]
         for t in range(tiles)
     ]
@@ -163,9 +163,9 @@
                 sbuf[c, begin + k, pl.ds(y, span, stride=ny), :] = part[:, k * 128 : (k + 1) * 128]
 
     def first_x(t):
-        for y in range(0, ny, 2):
-            load_v[t][y // 2].wait()
-            for k in (y, y + 1):
+        for y in range(0, ny, 4):
+            load_v[t][y // 4].wait()
+            for k in range(y, y + 4):
                 high, low = split(vbuf[t * per : (t + 1) * per, k].reshape(128, nx))
                 vhi[k, t * 128 : (t + 1) * 128] = high
                 vlo[k, t * 128 : (t + 1) * 128] = low
@@ -351,7 +351,7 @@
             pltpu.SMEM((nx,), F32),
             pltpu.VMEM((1, full_y), F32),
             pltpu.VMEM((1, full_z), F32),
-            dma((tiles, ny // 2)), dma((7,)),
+            dma((tiles, ny // 4)), dma((7,)),
             dma((1,)), dma((CYCLE * tiles,)), dma((1,)), dma((CYCLE * tiles,)),
         ],
         compiler_params=pltpu.CompilerParams(
@@ -370,7 +370,7 @@
         out_shape=jax.ShapeDtypeStruct((fields, share_x, share_y, full_z), F32),
         in_specs=[vector] * 5,
         out_specs=pl.BlockSpec(memory_space=pl.ANY),
-        scratch_shapes=[pltpu.VMEM((fields, share_y, full_z), F32), dma((2 * fields,))],
+        scratch_shapes=[pltpu.VMEM((fields, share_y, full_z), F32), dma((fields + 1,))],
         compiler_params=pltpu.CompilerParams(vmem_limit_bytes=8 << 20),
     )(*made)
 

time: 64.2 us -> 64.5 us (level)
  no operation moved by 1% of the time
where the time goes in v9:
time: 64.5 us; the launch traced here: 63.5 us
  Pallas kernels  63.5 us (98%)
    pallas_call x1, Pallas kernels, on_device(): pl.pallas_call(functools.partial(kernel, nn, nd), out_shape=(jax.ShapeDty...  61.4 us
    pallas_call x1, Pallas kernels, on_device(): pl.pallas_call(functools.partial(finish, nz), out_shape=jax.ShapeDtypeStr...  2.04 us

profile of v9, /device:TPU:0, one launch (start us, length us, event | category | flops | bytes accessed | tf_op | source)
XLA Modules:
  0.0 63.5 jit_solution(9888544686624890892)
XLA Ops:
  0.0 61.4 %shard_map.73 = (f32[4,16,64,256]{3,2,1,0:T(8,128)S(1)}, f32[2,4,64,128]{3,2,1,0:T(8,128)S(1)}, bf16[2,256,256]{2,1,0:T(8,128)(2,1)S(1)}, f32[64,256]{1,0:T(8,128)S(1)}, f32[16,256]{1,0:T(8,128)S(1)}) custom-call(f32[4,8,64,512]{3,2,1,0:T(8,128)} %bitcast.3, bf16[2,512,512]{2,1,0:T(8,128)(2,1)} %constant.4.clone.hx_hbm, ...), custom_call_target="tpu_custom_call" | custom-call | tf_op jit(solution)/shard_map/pallas_call | solution.py:328
  61.4 2.0 %shard_map.74 = f32[4,16,64,256]{3,2,1,0:T(8,128)} custom-call(f32[4,16,64,256]{3,2,1,0:T(8,128)S(1)} %get-tuple-element.10.most, f32[2,4,64,128]{3,2,1,0:T(8,128)S(1)} %get-tuple-element.11.last, bf16[2,256,256]{2,1,0:T(8,128)(2,1)S(1)} %get-tuple-element.12.table, f32[64,256]{1,0:T(8,128)S(1)} %get-tuple-element.13.weight, ...), custom_call_target="tpu_custom_call" | custom-call | tf_op jit(solution)/shard_map/pallas_call | solution.py:368
